TPU v7x, 128 devices: a whole 4x4x4 slice. The times are simulated.
128 devices in a mesh: wa: 8 (over z, core), bl: 16 (over x, y).
Axes of the slice: x: 4, y: 4, z: 4, core: 2. Of those that a mesh axis runs over, the one named last changes fastest.
Arguments:
- visibilities: float32 [8, 32, 2, 128], P('wa', 'bl'), may hold values from -6 to 6
- weights: float32 [8, 32, 128], P('wa', 'bl'), may hold values from 0.25 to 4
- cell_index: int32 [8, 32, 128], P('wa', 'bl'), may hold values from 0 to 1048575
- kernel_index: int32 [8, 32, 128], P('wa', 'bl'), may hold values from 0 to 255
- layer_index: int32 [8, 32, 128], P('wa', 'bl'), may hold values from 0 to 1
- tile_counts: int32 [8, 32], P('wa', 'bl'), may hold values from 1 to 128
- kernel_table: float32 [16, 8], replicated, may hold values from 0.05 to 0.3
- layer_depth: float32 [16], P('wa'), may hold values from -150 to 150
Outputs:
- image: float32 [1024, 1024], P('wa', 'bl')
All inputs are finite; a program needn't handle non-finite values.
Results may differ from a plain program's by a relative error of at most 0.0003.
Values sent between devices are 32-bit elements; how exact they have to be, the bound alone decides.
A program may use at most 128 MiB of HBM per device.

v0:
```python
import functools

import jax
import jax.numpy as jnp
import numpy as np
from jax import lax
from jax.experimental import pallas as pl
from jax.experimental.pallas import tpu as pltpu
from jax.sharding import PartitionSpec as P

GRID = 1024
SUPPORT = 8
OVERSAMPLE = 16
STRIP = 64
SLOTS = 256
FIELD = 0.6
NT = (((1,), (1,)), ((), ()))
NN = (((1,), (0,)), ((), ()))
TN = (((0,), (0,)), ((), ()))
F32 = jnp.float32
BF16 = jnp.bfloat16
I32 = jnp.int32


def turn_series():
    u = 0.125 * (1.0 - np.cos(np.pi * (np.arange(400) + 0.5) / 400))
    f = np.sqrt(u)
    out = []
    for values in (np.sin(2 * np.pi * f) / f, np.cos(2 * np.pi * f)):
        fit = np.polynomial.Chebyshev.fit(u, values, 7, domain=[0, 0.25])
        out.append([float(c) for c in fit.convert(kind=np.polynomial.Polynomial).coef])
    return out


SIN_TERMS, COS_TERMS = turn_series()


def horner(terms, u):
    total = jnp.full_like(u, terms[-1])
    for term in terms[-2::-1]:
        total = total * u + term
    return total


def turn_trig(turns):
    f = turns - jnp.floor(turns + 0.5)
    u = f * f
    return horner(COS_TERMS, u), f * horner(SIN_TERMS, u)


def split(value):
    high = value.astype(BF16)
    return high, (value - high.astype(F32)).astype(BF16)


def iota(shape, dim):
    return lax.broadcasted_iota(I32, shape, dim)


def dot(a, b, dims=NN, precision=None):
    return lax.dot_general(a, b, dims, precision=precision, preferred_element_type=F32)


def dft_tables():
    x = np.arange(256)[None, :, None] * 4 + np.arange(4)[:, None, None]
    angle = 2 * np.pi * ((x * np.arange(256)[None, None, :]) % GRID) / GRID
    table = np.concatenate([np.cos(angle), np.sin(angle)], axis=1).astype(np.float32)
    high = table.astype(jnp.bfloat16)
    low = (table - high.astype(np.float32)).astype(jnp.bfloat16)
    return high, low


def slot_rows(vis, weights, cell, kern, layer, counts):
    lane = iota((1, 128), 1)
    tiles = []
    for t in range(2):
        used = jnp.where(lane < counts[t], weights[t : t + 1], 0.0)
        tiles.append(
            jnp.concatenate(
                [
                    vis[t, 0:1] * used,
                    vis[t, 1:2] * used,
                    used,
                    cell[t : t + 1].astype(F32),
                    kern[t : t + 1].astype(F32),
                    layer[t : t + 1].astype(F32),
                    jnp.zeros((2, 128), F32),
                ],
                axis=0,
            )
        )
    return jnp.concatenate(tiles, axis=1)


def make_tables(first_y, table):
    lane = iota((STRIP, 256), 1)
    y = first_y + iota((STRIP, 256), 0)
    low5 = lane & 31
    step = jnp.where(lane < 64, 32 * low5, low5)
    turns = ((y * step) & (GRID - 1)).astype(F32) * (1.0 / GRID)
    c, s = turn_trig(turns)
    pieces = []
    for first in (0, 64):
        for value in (c, s):
            high, low = split(value)
            high, low = high.astype(F32), low.astype(F32)
            in_high = (lane >= first) & (lane < first + 32)
            in_low = (lane >= first + 32) & (lane < first + 64)
            pieces.append(jnp.where(in_high, high, jnp.where(in_low, low, 0.0)))
    wide = iota((OVERSAMPLE, 256), 1)
    pick = ((wide & 15) == iota((OVERSAMPLE, 256), 0)).astype(F32)
    spread = dot(table, pick, TN, lax.Precision.HIGHEST)
    offset = iota((STRIP, SUPPORT), 1) - SUPPORT // 2
    yy = first_y + iota((STRIP, SUPPORT), 0)
    turns = ((yy * offset) & (GRID - 1)).astype(F32) * (1.0 / GRID)
    for value in turn_trig(turns):
        factor = dot(value, spread, NN, lax.Precision.HIGHEST)
        high, low = split(factor)
        high, low = high.astype(F32), low.astype(F32)
        in_high = (lane >= 128) & (lane < 144)
        in_low = (lane >= 144) & (lane < 160)
        pieces.append(jnp.where(in_high, high, jnp.where(in_low, low, 0.0)))
    lane8 = iota((SUPPORT, 256), 1)
    own = (lane8 >= 160) & (lane8 < 176)
    high, low = split(spread)
    pieces.append(jnp.where(own, high.astype(F32), 0.0))
    pieces.append(jnp.where(own, low.astype(F32), 0.0))
    return jnp.concatenate(pieces, axis=0).astype(BF16)


def make_screen(first_y, depths, cos_ref, sin_ref):
    lane = iota((256, 128), 1)
    y = first_y + (lane & (STRIP - 1))
    yc = (y - GRID // 2).astype(F32) * (FIELD / GRID)
    depth = jnp.where(lane < STRIP, depths[0], depths[1])
    for xi in range(4):
        x = 4 * iota((256, 128), 0) + xi
        xc = (x - GRID // 2).astype(F32) * (FIELD / GRID)
        term = jnp.sqrt(1.0 - xc * xc - yc * yc) - 1.0
        c, s = turn_trig(depth * term)
        cos_ref[xi] = c
        sin_ref[xi] = s


def add_chunk(data, tables_ref, high_ref, low_ref, acc_ref):
    wr, wi = data[0:1], data[1:2]
    cell = data[3:4].astype(I32)
    kern = data[4:5].astype(I32)
    lay = data[5:6]
    row = cell >> 10
    col = cell & (GRID - 1)
    base = (row + (GRID - SUPPORT // 2)) & (GRID - 1)
    block, inner = base >> 4, base & 15

    def onehot(line, count):
        return (iota((count, SLOTS), 0) == line).astype(F32).astype(BF16)

    hot1 = onehot(col >> 5, 32)
    hot0 = onehot(col & 31, 32)
    hotv = onehot(kern & 15, 16)
    hotu = onehot(kern >> 4, 16)
    hot = jnp.concatenate(
        [hot1, hot1, hot0, hot0, hotv, hotv, hotu, jnp.zeros((80, SLOTS), BF16)], axis=0
    )
    found = dot(tables_ref[...], hot)
    ar, ai, br, bi, kr, ki = (found[64 * i : 64 * i + 64] for i in range(6))
    ku_high, ku_low = found[384:392], found[392:400]
    vr, vi = wr * kr - wi * ki, wr * ki + wi * kr
    cr, ci = ar * br - ai * bi, ar * bi + ai * br
    pr, pi = vr * cr - vi * ci, vr * ci + vi * cr
    second = lay.astype(BF16)
    first = (1.0 - lay).astype(BF16)
    rh, rl = split(pr)
    ih, il = split(pi)
    v_high = jnp.concatenate([rh * first, rh * second, ih * first, ih * second], axis=0)
    v_low = jnp.concatenate([rl * first, rl * second, il * first, il * second], axis=0)

    d = iota((16, SLOTS), 0) - inner
    zero = jnp.zeros((16, SLOTS), F32)
    lows, highs = [zero, zero], [zero, zero]
    for a in range(SUPPORT):
        here, past = d == a, d == a - 16
        for i, ku in enumerate((ku_high, ku_low)):
            lows[i] = jnp.where(here, ku[a : a + 1], lows[i])
            highs[i] = jnp.where(past, ku[a : a + 1], highs[i])
    lows = [v.astype(BF16) for v in lows]
    highs = [v.astype(BF16) for v in highs]
    blk = jnp.broadcast_to(block.astype(F32), (16, SLOTS)).astype(BF16)
    nxt = jnp.broadcast_to(((block + 1) & 63).astype(F32), (16, SLOTS)).astype(BF16)
    none = jnp.zeros((16, SLOTS), BF16)
    for q in range(64):
        at = blk == jnp.asarray(q, BF16)
        after = nxt == jnp.asarray(q, BF16)
        high_ref[16 * q : 16 * q + 16] = jnp.where(at, lows[0], jnp.where(after, highs[0], none))
        low_ref[16 * q : 16 * q + 16] = jnp.where(at, lows[1], jnp.where(after, highs[1], none))
    acc_ref[...] += (
        dot(high_ref[...], v_high, NT) + dot(high_ref[...], v_low, NT) + dot(low_ref[...], v_high, NT)
    )


def transform(acc_ref, fh_ref, fl_ref, cos_ref, sin_ref, store):
    g = [acc_ref[256 * i : 256 * i + 256] for i in range(4)]
    s02, d02, s13, d13 = g[0] + g[2], g[0] - g[2], g[1] + g[3], g[1] - g[3]
    turned = jnp.concatenate([-d13[:, 128:], d13[:, :128]], axis=1)
    mixed = [s02 + s13, d02 + turned, s02 - s13, d02 - turned]
    lane = iota((256, 128), 1)
    for pair in range(2):
        sums = []
        for xi in (2 * pair, 2 * pair + 1):
            high, low = split(mixed[xi])
            fh, fl = fh_ref[xi], fl_ref[xi]
            p = dot(fh, high) + dot(fh, low) + dot(fl, high)
            re = p[:256, :128] - p[256:, 128:]
            im = p[256:, :128] + p[:256, 128:]
            scr = re * cos_ref[xi] - im * sin_ref[xi]
            sums.append(scr + pltpu.roll(scr, 64, 1))
        store(pair, jnp.where(lane < 64, sums[0], sums[1]))


def compute_kernel(buf_ref, table_ref, depth_ref, fh_ref, fl_ref, out_ref, sq_ref, tables_ref, high_ref, low_ref, acc_ref, cos_ref, sin_ref):
    first_y = lax.axis_index("bl") * STRIP
    tables_ref[...] = make_tables(first_y, table_ref[...])
    make_screen(first_y, (depth_ref[0], depth_ref[1]), cos_ref, sin_ref)
    acc_ref[...] = jnp.zeros_like(acc_ref)

    def step(k, squares):
        data = buf_ref[k]
        add_chunk(data, tables_ref, high_ref, low_ref, acc_ref)
        return squares + data[2:3] * data[2:3]

    squares = lax.fori_loop(0, 16, step, jnp.zeros((1, SLOTS), F32))
    sq_ref[...] = jnp.broadcast_to(squares, (8, SLOTS))

    def store(pair, value):
        out_ref[pair] = value

    transform(acc_ref, fh_ref, fl_ref, cos_ref, sin_ref, store)


def body(visibilities, weights, cell_index, kernel_index, layer_index, tile_counts, kernel_table, layer_depth):
    rows = slot_rows(visibilities[0], weights[0], cell_index[0], kernel_index[0], layer_index[0], tile_counts[0])
    buf = lax.all_to_all(jnp.broadcast_to(rows[None], (16, 8, SLOTS)), "bl", 0, 0, tiled=True)
    fh, fl = dft_tables()
    vmem = pl.BlockSpec(memory_space=pltpu.VMEM)
    packed, squares = pl.pallas_call(
        compute_kernel,
        out_shape=(jax.ShapeDtypeStruct((2, 256, 128), F32), jax.ShapeDtypeStruct((8, SLOTS), F32)),
        in_specs=[vmem, vmem, pl.BlockSpec(memory_space=pltpu.SMEM), vmem, vmem],
        out_specs=(vmem, vmem),
        scratch_shapes=[
            pltpu.VMEM((400, 256), BF16),
            pltpu.VMEM((GRID, SLOTS), BF16),
            pltpu.VMEM((GRID, SLOTS), BF16),
            pltpu.VMEM((GRID, 256), F32),
            pltpu.VMEM((4, 256, 128), F32),
            pltpu.VMEM((4, 256, 128), F32),
        ],
    )(buf, kernel_table, layer_depth, jnp.asarray(fh), jnp.asarray(fl))
    total = jnp.sum(squares[0])
    blocks = packed.reshape(2, 8, 32, 128).transpose(1, 0, 2, 3).reshape(8, 64, 128)
    blocks = jnp.concatenate([blocks, jnp.full((8, 8, 128), total)], axis=1)
    got = lax.all_to_all(blocks, "wa", 0, 0, tiled=True).sum(axis=0)
    image = got[:64].reshape(2, 32, 2, 64).transpose(1, 0, 2, 3).reshape(128, 64)
    return image / jnp.sqrt(got[64, 0])


def solution(mesh):
    return jax.shard_map(
        body,
        mesh=mesh,
        in_specs=(
            P("wa", "bl", None, None),
            P("wa", "bl", None),
            P("wa", "bl", None),
            P("wa", "bl", None),
            P("wa", "bl", None),
            P("wa", "bl"),
            P(),
            P("wa"),
        ),
        out_specs=P("wa", "bl"),
        check_vma=False,
    )
```

profile of v0, /device:TPU:1, one launch (start us, length us, event | category | flops | bytes accessed | tf_op | source)
XLA Modules:
  0.0 59.6 jit_solution(10412766507367826748)
XLA Ops:
  0.0 0.0 copy-start.3
  0.0 0.8 %convert_bitcast_fusion.5 = (f32[1,128]{1,0:T(1,128)S(1)}, f32[1,128]{1,0:T(1,128)S(1)}) fusion(s32[1,2,128]{2,1,0:T(2,128)} %param.12), kind=kLoop, calls=%fused_computation.18 | loop fusion | flops 256 | bytes 2048 | tf_op jit(solution)/shard_map/convert_element_type | solution.py:84
  0.8 0.0 copy-done.3
  0.8 0.6 %fusion.4 = (s32[1,1]{1,0:T(1,128)}, s32[1,1]{1,0:T(1,128)}) fusion(s32[1,2]{1,0:T(1,128)S(1)} %copy-done.3), kind=kLoop, calls=%fused_computation.19 | loop fusion | bytes 16 | tf_op jit(solution)/shard_map/slice | solution.py:77
  1.4 0.0 copy-start.2
  1.4 0.0 copy-start.4
  1.4 0.7 %copy-done.2 = f32[1,2,2,128]{3,2,1,0:T(2,128)S(1)} copy-done((f32[1,2,2,128]{3,2,1,0:T(2,128)S(1)}, f32[1,2,2,128]{3,2,1,0:T(2,128)}, u32[]{:S(2)}) %copy-start.2) | copy-done | bytes 2072
  2.1 0.0 copy-done.4
  2.1 1.3 %fusion.2 = (f32[1,128]{1,0:T(1,128)S(1)}, f32[1,128]{1,0:T(1,128)S(1)}, f32[1,128]{1,0:T(1,128)S(1)}, f32[1,128]{1,0:T(1,128)S(1)}) fusion(f32[2,2,128]{2,1,0:T(2,128)S(1)} %bitcast.48, f32[1,2,128]{2,1,0:T(2,128)S(1)} %copy-done.4, s32[]{:T(128)} %bitcast.2, s32[]{:T(128)} %bitcast.9), kind=kLoop, calls=%fused_computation.10 | loop fusion | flops 768 | bytes 4104 | tf_op jit(solution)/shard_map/mul | solution.py:82
  3.4 0.0 copy-start.5
  3.4 0.0 copy-start.6
  3.4 0.6 %copy-done.5 = s32[1,2,128]{2,1,0:T(2,128)S(1)} copy-done((s32[1,2,128]{2,1,0:T(2,128)S(1)}, s32[1,2,128]{2,1,0:T(2,128)}, u32[]{:S(2)}) %copy-start.5) | copy-done | bytes 1048
  4.1 0.0 copy-done.6
  4.1 0.7 %broadcast_in_dim.13 = f32[16,8,256]{2,1,0:T(8,128)} broadcast(f32[8,256]{1,0:T(8,128)S(1)} %pad_maximum_fusion), dimensions={1,2} | broadcast | bytes 139264 | tf_op jit(solution)/shard_map/broadcast_in_dim | solution.py:242
  4.8 0.0 copy-start.1
  4.8 7.7 %all-to-all-start = ((f32[16,8,256]{2,1,0:T(8,128)}), f32[16,8,256]{2,1,0:T(8,128)S(1)}, u32[]{:S(2)}, u32[]{:S(2)}) async-start(f32[16,8,256]{2,1,0:T(8,128)} %broadcast_in_dim.13), calls=%async_computation | async-start | bytes 262144 | tf_op jit(solution)/shard_map/all_to_all | solution.py:242
  12.5 0.0 copy-done.1
  12.5 0.7 %copy.12.table_ref = f32[16,8]{1,0:T(8,128)} copy(f32[16,8]{0,1:T(8,128)S(1)} %copy-done.1) | data formatting | bytes 1024 | tf_op args[6]
  13.2 6.2 %all-to-all-done.buf_ref = f32[16,8,256]{2,1,0:T(8,128)S(1)} async-done(((f32[16,8,256]{2,1,0:T(8,128)}), f32[16,8,256]{2,1,0:T(8,128)S(1)}, u32[]{:S(2)}, u32[]{:S(2)}) %all-to-all-start) | async-done | bytes 131104 | tf_op jit(solution)/shard_map/all_to_all | solution.py:242
  19.4 0.0 copy-start
  19.4 0.6 %copy-done = f32[16,8,256]{2,1,0:T(8,128)} copy-done((f32[16,8,256]{2,1,0:T(8,128)}, f32[16,8,256]{2,1,0:T(8,128)S(1)}, u32[]{:S(2)}) %copy-start) | copy-done | bytes 131096
  20.0 20.2 %shard_map.100 = (f32[2,256,128]{2,1,0:T(8,128)}, f32[8,256]{1,0:T(8,128)}) custom-call(f32[16,8,256]{2,1,0:T(8,128)} %copy-done, f32[16,8]{1,0:T(8,128)} %copy.12.table_ref, f32[2]{0:T(128)} %depth_ref.1, bf16[4,512,256]{2,1,0:T(8,128)(2,1)} %constant.2.clone.fh_ref, bf16[4,512,256]{2,1,0:T(8,128)(2,1)} %constant.8.clone.fl_ref), custom_call_target="tpu_custom_call" | custom-call | tf_op jit(solution)/shard_map/pallas_call | solution.py:245
  40.3 1.3 %slice_reduce_fusion = f32[]{:T(128)} fusion(f32[8,256]{1,0:T(8,128)} %get-tuple-element.8), kind=kLoop, calls=%fused_computation.4 | loop fusion | flops 255 | bytes 1028 | tf_op jit(solution)/shard_map/reduce_sum | solution.py:259
  41.6 1.0 %copy.13 = f32[2,8,32,128]{3,2,0,1:T(8,128)S(1)} copy(f32[2,8,32,128]{3,2,1,0:T(8,128)} %bitcast.45) | data formatting | bytes 524288 | tf_op jit(solution)/shard_map/reshape | solution.py:260
  42.5 0.7 %concatenate.15 = f32[8,72,128]{2,1,0:T(8,128)S(1)} pad(f32[8,64,128]{2,1,0:T(8,128)S(1)} %bitcast.44, f32[]{:T(128)} %slice_reduce_fusion), padding=0_0x0_8x0_0 | pad | bytes 557060 | tf_op jit(solution)/shard_map/concatenate | solution.py:261
  43.2 14.3 %all_to_all.10 = f32[8,72,128]{2,1,0:T(8,128)S(1)} all-to-all(f32[8,72,128]{2,1,0:T(8,128)S(1)} %concatenate.15), channel_id=1, replica_groups=mesh['wa'=8,'bl'=16] {'wa'}, dimensions={0} | all-to-all | bytes 589824 | tf_op jit(solution)/shard_map/all_to_all | solution.py:262
  57.6 0.5 slice.89
  58.8 0.1 div.17
  58.9 0.7 %copy.15 = f32[128,64]{0,1:T(8,128)} copy(f32[128,64]{1,0:T(8,128)S(1)} %bitcast.47) | data formatting | bytes 65536 | tf_op jit(solution)/shard_map/div | solution.py:264
  (9 shorter events, 0.1 us)
Async XLA Ops:
  0.0 0.8 %copy-start.3 = (s32[1,2]{1,0:T(1,128)S(1)}, s32[1,2]{1,0:T(1,128)}, u32[]{:S(2)}) copy-start(s32[1,2]{1,0:T(1,128)} %param.15) | copy-start | bytes 28
  1.4 0.7 %copy-start.2 = (f32[1,2,2,128]{3,2,1,0:T(2,128)S(1)}, f32[1,2,2,128]{3,2,1,0:T(2,128)}, u32[]{:S(2)}) copy-start(f32[1,2,2,128]{3,2,1,0:T(2,128)} %param.10) | copy-start | bytes 6148
  1.4 0.7 %copy-start.4 = (f32[1,2,128]{2,1,0:T(2,128)S(1)}, f32[1,2,128]{2,1,0:T(2,128)}, u32[]{:S(2)}) copy-start(f32[1,2,128]{2,1,0:T(2,128)} %param.11) | copy-start | bytes 3076
  3.4 0.7 %copy-start.5 = (s32[1,2,128]{2,1,0:T(2,128)S(1)}, s32[1,2,128]{2,1,0:T(2,128)}, u32[]{:S(2)}) copy-start(s32[1,2,128]{2,1,0:T(2,128)} %param.14) | copy-start | bytes 3076
  3.4 0.7 %copy-start.6 = (s32[1,2,128]{2,1,0:T(2,128)S(1)}, s32[1,2,128]{2,1,0:T(2,128)}, u32[]{:S(2)}) copy-start(s32[1,2,128]{2,1,0:T(2,128)} %param.13) | copy-start | bytes 3076
  4.8 7.7 %copy-start.1 = (f32[16,8]{0,1:T(8,128)S(1)}, f32[16,8]{0,1:T(8,128)}, u32[]{:S(2)}) copy-start(f32[16,8]{0,1:T(8,128)} %param.16) | copy-start | bytes 1540
  4.8 14.6 %all-to-all-start = ((f32[16,8,256]{2,1,0:T(8,128)}), f32[16,8,256]{2,1,0:T(8,128)S(1)}, u32[]{:S(2)}, u32[]{:S(2)}) async-start(f32[16,8,256]{2,1,0:T(8,128)} %broadcast_in_dim.13), calls=%async_computation | async-start | bytes 262144 | tf_op jit(solution)/shard_map/all_to_all | solution.py:242
  19.4 0.6 %copy-start = (f32[16,8,256]{2,1,0:T(8,128)}, f32[16,8,256]{2,1,0:T(8,128)S(1)}, u32[]{:S(2)}) copy-start(f32[16,8,256]{2,1,0:T(8,128)S(1)} %all-to-all-done.buf_ref) | copy-start | bytes 393220
where the time goes:
time: 60 us; the launch traced here: 59.6 us
  Pallas kernels  20.2 us (34%)
  blocking collectives  14.3 us (24%)
  starting transfers between devices  7.7 us (13%)
  local copies, waits for them, and re-layouts  6.98 us (12%)
  waiting for transfers between devices  6.18 us (10%)
  other arithmetic  3.38 us (6%)
  between operations  0.8 us (1%)
    pallas_call x1, Pallas kernels, body(): pl.pallas_call(compute_kernel, out_shape=(jax.ShapeDtypeStruct((2, 256, 1...  20.2 us
    all_to_all x1, blocking collectives, body(): got = lax.all_to_all(blocks, 'wa', 0, 0, tiled=True).sum(axis=0)  14.3 us
    all_to_all x1, starting transfers between devices, body(): lax.all_to_all(jnp.broadcast_to(rows[None], (16, 8, SLOTS)), 'bl', 0, 0,...  7.7 us
    all_to_all x1, waiting for transfers between devices, body(): lax.all_to_all(jnp.broadcast_to(rows[None], (16, 8, SLOTS)), 'bl', 0, 0,...  6.18 us
    unnamed x15, local copies, waits for them, and re-layouts  2.68 us
    reduce_sum x1, other arithmetic, body(): total = jnp.sum(squares[0])  1.3 us
    mul x1, other arithmetic, slot_rows(): vis[t, 1:2] * used  1.27 us
  transfers between devices with their start and end apart: 1, of which 1 were waited for; matrix products, arithmetic and copies ran while one was open for 1% of the time, Pallas kernels for 0%

commit v1 on v0

--- a/solution.py
+++ b/solution.py
@@ -1,5 +1,3 @@
-import functools
-
 import jax
 import jax.numpy as jnp
 import numpy as np
@@ -109,7 +107,7 @@
             pieces.append(jnp.where(in_high, high, jnp.where(in_low, low, 0.0)))
     wide = iota((OVERSAMPLE, 256), 1)
     pick = ((wide & 15) == iota((OVERSAMPLE, 256), 0)).astype(F32)
-    spread = dot(table, pick, TN, lax.Precision.HIGHEST)
+    spread = dot(table, pick, NN, lax.Precision.HIGHEST)
     offset = iota((STRIP, SUPPORT), 1) - SUPPORT // 2
     yy = first_y + iota((STRIP, SUPPORT), 0)
     turns = ((yy * offset) & (GRID - 1)).astype(F32) * (1.0 / GRID)
@@ -217,51 +215,155 @@
         store(pair, jnp.where(lane < 64, sums[0], sums[1]))
 
 
-def compute_kernel(buf_ref, table_ref, depth_ref, fh_ref, fl_ref, out_ref, sq_ref, tables_ref, high_ref, low_ref, acc_ref, cos_ref, sin_ref):
-    first_y = lax.axis_index("bl") * STRIP
+def mesh_offsets():
+    near = lambda d: min(d, 4 - d)
+    return sorted(((dx, dy) for dx in range(4) for dy in range(4)), key=lambda o: near(o[0]) + near(o[1]))
+
+
+OFFSETS = mesh_offsets()
+MESH = pl.DeviceIdType.MESH
+
+
+def kernel(
+    counts_ref, depth_ref, vis_ref, weights_ref, cell_ref, kern_ref, layer_ref, table_ref, fh_hbm, fl_hbm,
+    out_ref,
+    buf, tables_ref, high_ref, low_ref, acc_ref, cos_ref, sin_ref, fh_ref, fl_ref, send0, send1, got0, got1, rows_ref,
+    table_sem, slot_send, slot_recv, part_send, part_recv,
+):
+    bl, wa = lax.axis_index("bl"), lax.axis_index("wa")
+    bx, by = bl // 4, bl % 4
+    strips = [((bx + dx) % 4) * 4 + (by + dy) % 4 for dx, dy in OFFSETS]
+    groups = [(wa + j) % 8 for j in range(8)]
+
+    barrier = pltpu.get_barrier_semaphore()
+    for k in range(1, 16):
+        pl.semaphore_signal(barrier, inc=1, device_id={"bl": strips[k]}, device_id_type=MESH)
+    for j in range(1, 8):
+        pl.semaphore_signal(barrier, inc=1, device_id={"wa": groups[j]}, device_id_type=MESH)
+    loads = [
+        pltpu.make_async_copy(fh_hbm, fh_ref, table_sem.at[0]),
+        pltpu.make_async_copy(fl_hbm, fl_ref, table_sem.at[1]),
+    ]
+    for load in loads:
+        load.start()
+
+    buf[0] = slot_rows(
+        vis_ref[0], weights_ref[0], cell_ref[0], kern_ref[0], layer_ref[0], (counts_ref[0, 0], counts_ref[0, 1])
+    )
+    first_y = bl * STRIP
     tables_ref[...] = make_tables(first_y, table_ref[...])
     make_screen(first_y, (depth_ref[0], depth_ref[1]), cos_ref, sin_ref)
     acc_ref[...] = jnp.zeros_like(acc_ref)
 
+    pl.semaphore_wait(barrier, 22)
+
+    def slot_copy(k, strip):
+        return pltpu.make_async_remote_copy(
+            src_ref=buf.at[0],
+            dst_ref=buf.at[k],
+            send_sem=slot_send.at[k],
+            recv_sem=slot_recv.at[k],
+            device_id={"bl": strip},
+            device_id_type=MESH,
+        )
+
+    copies = [slot_copy(k, strips[k]) for k in range(1, 16)]
+    for copy in copies:
+        copy.start()
+
+    own = buf[0]
+    add_chunk(own, tables_ref, high_ref, low_ref, acc_ref)
+
     def step(k, squares):
-        data = buf_ref[k]
+        slot_copy(k, strips[1]).wait_recv()
+        data = buf[k]
         add_chunk(data, tables_ref, high_ref, low_ref, acc_ref)
         return squares + data[2:3] * data[2:3]
 
-    squares = lax.fori_loop(0, 16, step, jnp.zeros((1, SLOTS), F32))
-    sq_ref[...] = jnp.broadcast_to(squares, (8, SLOTS))
+    squares = lax.fori_loop(1, 16, step, own[2:3] * own[2:3])
+    squares = squares[:, :128] + squares[:, 128:]
+    for copy in copies:
+        copy.wait_send()
+    for load in loads:
+        load.wait()
+
+    parts = ((send0, got0), (send1, got1))
+
+    def part_copy(pair, j):
+        source, target = parts[pair]
+        return pltpu.make_async_remote_copy(
+            src_ref=source.at[groups[j]],
+            dst_ref=target.at[j],
+            send_sem=part_send.at[pair, j],
+            recv_sem=part_recv.at[pair, j],
+            device_id={"wa": groups[j]},
+            device_id_type=MESH,
+        )
+
+    sent = []
 
     def store(pair, value):
-        out_ref[pair] = value
+        parts[pair][0][:, 0:32] = value.reshape(8, 32, 128)
+        if pair == 0:
+            send0[:, 32:40] = jnp.broadcast_to(squares[None], (8, 8, 128))
+        for j in range(1, 8):
+            copy = part_copy(pair, j)
+            copy.start()
+            sent.append(copy)
 
     transform(acc_ref, fh_ref, fl_ref, cos_ref, sin_ref, store)
+    norm = None
+    for pair in range(2):
+        source, target = parts[pair]
+        total = source[wa]
+        for j in range(1, 8):
+            part_copy(pair, j).wait_recv()
+            total = total + target[j]
+        if pair == 0:
+            norm = lax.rsqrt(jnp.sum(total[32:33], axis=1, keepdims=True))
+        image = total[0:32] * norm
+        rows_ref[pl.ds(2 * pair, 32, stride=4), :] = image
+        rows_ref[pl.ds(2 * pair + 1, 32, stride=4), :] = pltpu.roll(image, 64, 1)
+    out_ref[...] = rows_ref[...].T[:STRIP]
+    for copy in sent:
+        copy.wait_send()
 
 
 def body(visibilities, weights, cell_index, kernel_index, layer_index, tile_counts, kernel_table, layer_depth):
-    rows = slot_rows(visibilities[0], weights[0], cell_index[0], kernel_index[0], layer_index[0], tile_counts[0])
-    buf = lax.all_to_all(jnp.broadcast_to(rows[None], (16, 8, SLOTS)), "bl", 0, 0, tiled=True)
     fh, fl = dft_tables()
     vmem = pl.BlockSpec(memory_space=pltpu.VMEM)
-    packed, squares = pl.pallas_call(
-        compute_kernel,
-        out_shape=(jax.ShapeDtypeStruct((2, 256, 128), F32), jax.ShapeDtypeStruct((8, SLOTS), F32)),
-        in_specs=[vmem, vmem, pl.BlockSpec(memory_space=pltpu.SMEM), vmem, vmem],
-        out_specs=(vmem, vmem),
+    smem = pl.BlockSpec(memory_space=pltpu.SMEM)
+    far = pl.BlockSpec(memory_space=pl.ANY)
+    return pl.pallas_call(
+        kernel,
+        out_shape=jax.ShapeDtypeStruct((STRIP, 128), F32),
+        in_specs=[smem, smem] + [vmem] * 6 + [far, far],
+        out_specs=vmem,
         scratch_shapes=[
+            pltpu.VMEM((16, 8, SLOTS), F32),
             pltpu.VMEM((400, 256), BF16),
             pltpu.VMEM((GRID, SLOTS), BF16),
             pltpu.VMEM((GRID, SLOTS), BF16),
             pltpu.VMEM((GRID, 256), F32),
             pltpu.VMEM((4, 256, 128), F32),
             pltpu.VMEM((4, 256, 128), F32),
+            pltpu.VMEM((4, 512, 256), BF16),
+            pltpu.VMEM((4, 512, 256), BF16),
+            pltpu.VMEM((8, 40, 128), F32),
+            pltpu.VMEM((8, 32, 128), F32),
+            pltpu.VMEM((8, 40, 128), F32),
+            pltpu.VMEM((8, 32, 128), F32),
+            pltpu.VMEM((128, 128), F32),
+            pltpu.SemaphoreType.DMA((2,)),
+            pltpu.SemaphoreType.DMA((16,)),
+            pltpu.SemaphoreType.DMA((16,)),
+            pltpu.SemaphoreType.DMA((2, 8)),
+            pltpu.SemaphoreType.DMA((2, 8)),
         ],
-    )(buf, kernel_table, layer_depth, jnp.asarray(fh), jnp.asarray(fl))
-    total = jnp.sum(squares[0])
-    blocks = packed.reshape(2, 8, 32, 128).transpose(1, 0, 2, 3).reshape(8, 64, 128)
-    blocks = jnp.concatenate([blocks, jnp.full((8, 8, 128), total)], axis=1)
-    got = lax.all_to_all(blocks, "wa", 0, 0, tiled=True).sum(axis=0)
-    image = got[:64].reshape(2, 32, 2, 64).transpose(1, 0, 2, 3).reshape(128, 64)
-    return image / jnp.sqrt(got[64, 0])
+        compiler_params=pltpu.CompilerParams(
+            collective_id=0, has_side_effects=True, vmem_limit_bytes=60 * 1024 * 1024
+        ),
+    )(tile_counts, layer_depth, visibilities, weights, cell_index, kernel_index, layer_index, kernel_table.T, jnp.asarray(fh), jnp.asarray(fl)).T
 
 
 def solution(mesh):

time: 60 us -> 34.8 us (0.58)
  blocking collectives: 14.3 us -> 0 us
  Pallas kernels: 20.2 us -> 33.2 us
  starting transfers between devices: 7.7 us -> 0 us
  waiting for transfers between devices: 6.18 us -> 0 us
  local copies, waits for them, and re-layouts: 6.98 us -> 1.38 us
  other arithmetic: 3.38 us -> 0 us
  between operations: 0.8 us -> 0.01 us
    all_to_all x1 -> x0, blocking collectives: 14.3 us -> none  [body(): got = lax.all_to_all(blocks, 'wa', 0, 0, tiled=True).sum(axis=0)]
    pallas_call x1, Pallas kernels: 20.2 us -> 33.2 us  [body(): pl.pallas_call(kernel, out_shape=jax.ShapeDtypeStruct((STRIP, 128), F32),...]
    all_to_all x1 -> x0, starting transfers between devices: 7.7 us -> none  [body(): lax.all_to_all(jnp.broadcast_to(rows[None], (16, 8, SLOTS)), 'bl', 0, 0,...]
    all_to_all x1 -> x0, waiting for transfers between devices: 6.18 us -> none  [body(): lax.all_to_all(jnp.broadcast_to(rows[None], (16, 8, SLOTS)), 'bl', 0, 0,...]
    reduce_sum x2 -> x0, other arithmetic: 1.32 us -> none  [the longest x1 1.3 us: body(): total = jnp.sum(squares[0])]
    unnamed x15 -> x1, local copies, waits for them, and re-layouts: 2.68 us -> 1.38 us
    mul x2 -> x0, other arithmetic: 1.28 us -> none  [the longest x1 1.27 us: slot_rows(): vis[t, 1:2] * used]
    slice x2 -> x0, local copies, waits for them, and re-layouts: 1.15 us -> none  [the longest x1 0.63 us: slot_rows(): used = jnp.where(lane < counts[t], weights[t:t + 1], 0.0)]
  transfers between devices with their start and end apart: 1 -> 0, of which waited for: 1 -> 0; matrix products, arithmetic and copies ran while one was open for 1% -> 0% of each run, Pallas kernels for 0% -> 0%
where the time goes in v1:
time: 34.8 us; the launch traced here: 34.6 us
  Pallas kernels  33.2 us (95%)
  local copies, waits for them, and re-layouts  1.38 us (4%)
    pallas_call x1, Pallas kernels, body(): pl.pallas_call(kernel, out_shape=jax.ShapeDtypeStruct((STRIP, 128), F32),...  33.2 us
    unnamed x1, local copies, waits for them, and re-layouts  1.38 us

profile of v1, /device:TPU:1, one launch (start us, length us, event | category | flops | bytes accessed | tf_op | source)
XLA Modules:
  0.0 34.6 jit_solution(8808137267678341778)
XLA Ops:
  0.0 33.2 %shard_map.100 = f32[64,128]{1,0:T(8,128)} custom-call(s32[1,2]{1,0:T(1,128)} %counts_ref.1, f32[2]{0:T(128)} %depth_ref.1, f32[1,2,2,128]{3,2,1,0:T(2,128)} %vis_ref.1, f32[1,2,128]{2,1,0:T(2,128)} %weights_ref.1, s32[1,2,128]{2,1,0:T(2,128)} %cell_ref.1, s32[1,2,128]{2,1,0:T(2,128)} %kern_ref.1, s32[1,2,128]{2,1,0:T(2,128)} %layer_ref.1, f32[8,16]{1,0:T(8,128)} %bitcast.3, ...), custom_call_target="tpu_custom_call" | custom-call | tf_op jit(solution)/shard_map/pallas_call | solution.py:337
  33.2 1.4 %copy.12 = f32[128,64]{0,1:T(8,128)} copy(f32[128,64]{0,1:T(8,128)} %bitcast.2) | data formatting | bytes 65536

commit v2 on v0

--- a/solution.py
+++ b/solution.py
@@ -14,6 +14,10 @@
 STRIP = 64
 SLOTS = 256
 FIELD = 0.6
+MIX = 0
+GROUPS = (1,2,3,3,3,3)
+MROWS = 256
+VMEM_MIB = 60
 NT = (((1,), (1,)), ((), ()))
 NN = (((1,), (0,)), ((), ()))
 TN = (((0,), (0,)), ((), ()))
@@ -109,7 +113,7 @@
             pieces.append(jnp.where(in_high, high, jnp.where(in_low, low, 0.0)))
     wide = iota((OVERSAMPLE, 256), 1)
     pick = ((wide & 15) == iota((OVERSAMPLE, 256), 0)).astype(F32)
-    spread = dot(table, pick, TN, lax.Precision.HIGHEST)
+    spread = dot(table, pick, NN, lax.Precision.HIGHEST)
     offset = iota((STRIP, SUPPORT), 1) - SUPPORT // 2
     yy = first_y + iota((STRIP, SUPPORT), 0)
     turns = ((yy * offset) & (GRID - 1)).astype(F32) * (1.0 / GRID)
@@ -142,7 +146,7 @@
         sin_ref[xi] = s
 
 
-def add_chunk(data, tables_ref, high_ref, low_ref, acc_ref):
+def slot_factors(data, tables_ref):
     wr, wi = data[0:1], data[1:2]
     cell = data[3:4].astype(I32)
     kern = data[4:5].astype(I32)
@@ -187,15 +191,32 @@
     highs = [v.astype(BF16) for v in highs]
     blk = jnp.broadcast_to(block.astype(F32), (16, SLOTS)).astype(BF16)
     nxt = jnp.broadcast_to(((block + 1) & 63).astype(F32), (16, SLOTS)).astype(BF16)
+    return v_high, v_low, lows, highs, blk, nxt
+
+
+def fill_operands(n, data, tables_ref, vh_ref, vl_ref, high_ref, low_ref):
     none = jnp.zeros((16, SLOTS), BF16)
+    lanes = slice(SLOTS * n, SLOTS * n + SLOTS)
+    v_high, v_low, lows, highs, blk, nxt = slot_factors(data, tables_ref)
+    vh_ref[:, lanes] = v_high
+    vl_ref[:, lanes] = v_low
     for q in range(64):
         at = blk == jnp.asarray(q, BF16)
         after = nxt == jnp.asarray(q, BF16)
-        high_ref[16 * q : 16 * q + 16] = jnp.where(at, lows[0], jnp.where(after, highs[0], none))
-        low_ref[16 * q : 16 * q + 16] = jnp.where(at, lows[1], jnp.where(after, highs[1], none))
-    acc_ref[...] += (
-        dot(high_ref[...], v_high, NT) + dot(high_ref[...], v_low, NT) + dot(low_ref[...], v_high, NT)
+        rows = slice(16 * q, 16 * q + 16)
+        high_ref[rows, lanes] = jnp.where(at, lows[0], jnp.where(after, highs[0], none))
+        low_ref[rows, lanes] = jnp.where(at, lows[1], jnp.where(after, highs[1], none))
+
+
+def add_rows(m, count, first, acc_ref, vh_ref, vl_ref, high_ref, low_ref):
+    lanes = slice(0, SLOTS * count)
+    rows = slice(m, m + MROWS)
+    added = (
+        dot(high_ref[rows, lanes], vh_ref[:, lanes], NT)
+        + dot(high_ref[rows, lanes], vl_ref[:, lanes], NT)
+        + dot(low_ref[rows, lanes], vh_ref[:, lanes], NT)
     )
+    acc_ref[rows] = added if first else acc_ref[rows] + added
 
 
 def transform(acc_ref, fh_ref, fl_ref, cos_ref, sin_ref, store):
@@ -217,51 +238,204 @@
         store(pair, jnp.where(lane < 64, sums[0], sums[1]))
 
 
-def compute_kernel(buf_ref, table_ref, depth_ref, fh_ref, fl_ref, out_ref, sq_ref, tables_ref, high_ref, low_ref, acc_ref, cos_ref, sin_ref):
-    first_y = lax.axis_index("bl") * STRIP
+def mesh_offsets():
+    near = lambda d: min(d, 4 - d)
+    return sorted(((dx, dy) for dx in range(4) for dy in range(4)), key=lambda o: near(o[0]) + near(o[1]))
+
+
+OFFSETS = mesh_offsets()
+MESH = pl.DeviceIdType.MESH
+
+
+def ORDER(fills, adds):
+    total = len(fills) + len(adds)
+    while fills or adds:
+        if fills and (not adds or MIX == 0 or len(fills) * MIX >= len(adds)):
+            fills.pop(0)()
+        else:
+            adds.pop(0)()
+
+
+def kernel(
+    counts_hbm, depth_hbm, vis_hbm, weights_hbm, cell_hbm, kern_hbm, layer_hbm, table_hbm, fh_hbm, fl_hbm,
+    out_ref,
+    counts_ref, depth_ref, vis_ref, weights_ref, cell_ref, kern_ref, layer_ref, table_ref, fh_ref, fl_ref,
+    buf, tables_ref, vh0, vl0, high0, low0, vh1, vl1, high1, low1, acc_ref, cos_ref, sin_ref,
+    send0, send1, half0, half1, red0, red1, got0, got1, rows_ref,
+    load_sem, slot_send, slot_recv, half_send, half_recv, part_send, part_recv,
+):
+    bl, wa = lax.axis_index("bl"), lax.axis_index("wa")
+    bx, by, z, core = bl // 4, bl % 4, wa // 2, wa % 2
+    strips = [{"bl": (bx + dx) % 4 * 4 + (by + dy) % 4} for dx, dy in OFFSETS]
+    z_peer = [{"wa": (z + d) % 4 * 2 + core} for d in range(4)]
+    sibling = {"wa": z * 2 + (1 - core)}
+
+    barrier = pltpu.get_barrier_semaphore()
+    for peer in strips[:0:-1] + z_peer[1:] + [sibling]:
+        pl.semaphore_signal(barrier, inc=1, device_id=peer, device_id_type=MESH)
+    sources = (vis_hbm, weights_hbm, cell_hbm, kern_hbm, layer_hbm, counts_hbm, depth_hbm, table_hbm, fh_hbm, fl_hbm)
+    targets = (vis_ref, weights_ref, cell_ref, kern_ref, layer_ref, counts_ref, depth_ref, table_ref, fh_ref, fl_ref)
+    loads = [pltpu.make_async_copy(a, b, load_sem.at[n]) for n, (a, b) in enumerate(zip(sources, targets))]
+    for load in loads:
+        load.start()
+    for load in loads[:6]:
+        load.wait()
+    buf[0] = slot_rows(
+        vis_ref[0], weights_ref[0], cell_ref[0], kern_ref[0], layer_ref[0], (counts_ref[0, 0], counts_ref[0, 1])
+    )
+    copies = [
+        pltpu.make_async_remote_copy(
+            src_ref=buf.at[0],
+            dst_ref=buf.at[k],
+            send_sem=slot_send.at[k],
+            recv_sem=slot_recv.at[k],
+            device_id=strips[k],
+            device_id_type=MESH,
+        )
+        for k in range(1, 16)
+    ]
+    pl.semaphore_wait(barrier, 19)
+    for copy in copies[::-1]:
+        copy.start()
+
+    first_y = bl * STRIP
+    loads[7].wait()
     tables_ref[...] = make_tables(first_y, table_ref[...])
+    operands = ((vh0, vl0, high0, low0), (vh1, vl1, high1, low1))
+    own = buf[0]
+    squares = own[2:3] * own[2:3]
+    fill_operands(0, own, tables_ref, *operands[0])
+    for m in range(0, GRID, MROWS):
+        add_rows(m, 1, True, acc_ref, *operands[0])
+    loads[6].wait()
     make_screen(first_y, (depth_ref[0], depth_ref[1]), cos_ref, sin_ref)
-    acc_ref[...] = jnp.zeros_like(acc_ref)
-
-    def step(k, squares):
-        data = buf_ref[k]
-        add_chunk(data, tables_ref, high_ref, low_ref, acc_ref)
-        return squares + data[2:3] * data[2:3]
-
-    squares = lax.fori_loop(0, 16, step, jnp.zeros((1, SLOTS), F32))
-    sq_ref[...] = jnp.broadcast_to(squares, (8, SLOTS))
+    k, ready = 1, 0
+    for n, count in enumerate(GROUPS):
+        for copy in copies[k - 1 : k - 1 + count]:
+            copy.wait_recv()
+        fills = []
+        for m in range(count):
+            data = buf[k + m]
+            squares = squares + data[2:3] * data[2:3]
+            fills.append(functools.partial(fill_operands, m, data, tables_ref, *operands[(n + 1) % 2]))
+        adds = [
+            functools.partial(add_rows, m, ready, False, acc_ref, *operands[n % 2])
+            for m in range(0, GRID if ready else 0, MROWS)
+        ]
+        ORDER(fills, adds)
+        k, ready = k + count, count
+    for m in range(0, GRID, MROWS):
+        add_rows(m, ready, False, acc_ref, *operands[len(GROUPS) % 2])
+    squares = squares[:, :128] + squares[:, 128:]
+    for copy in copies:
+        copy.wait_send()
+    for load in loads[8:]:
+        load.wait()
+
+    sends, halves, reds, gots = (send0, send1), (half0, half1), (red0, red1), (got0, got1)
+
+    def half_copy(pair):
+        return pltpu.make_async_remote_copy(
+            src_ref=sends[pair].at[1 - core],
+            dst_ref=halves[pair],
+            send_sem=half_send.at[pair],
+            recv_sem=half_recv.at[pair],
+            device_id=sibling,
+            device_id_type=MESH,
+        )
+
+    def part_copy(pair, d):
+        return pltpu.make_async_remote_copy(
+            src_ref=reds[pair].at[(z + d) % 4],
+            dst_ref=gots[pair].at[d],
+            send_sem=part_send.at[pair, d],
+            recv_sem=part_recv.at[pair, d],
+            device_id=z_peer[d],
+            device_id_type=MESH,
+        )
 
     def store(pair, value):
-        out_ref[pair] = value
+        for w in range(8):
+            sends[pair][w % 2, w // 2, 0:32] = value[32 * w : 32 * w + 32]
+        if pair == 0:
+            send0[:, :, 32:40] = jnp.broadcast_to(squares[None, None], (2, 4, 8, 128))
+        half_copy(pair).start()
 
     transform(acc_ref, fh_ref, fl_ref, cos_ref, sin_ref, store)
+    for pair in range(2):
+        half_copy(pair).wait_recv()
+        reds[pair][...] = sends[pair][core] + halves[pair][...]
+        for d in (2, 1, 3):
+            part_copy(pair, d).start()
+    norm = None
+    for pair in range(2):
+        total = reds[pair][z]
+        for d in (1, 3, 2):
+            part_copy(pair, d).wait_recv()
+            total = total + gots[pair][d]
+        if pair == 0:
+            norm = lax.rsqrt(jnp.sum(total[32:33], axis=1, keepdims=True))
+        image = total[0:32] * norm
+        rows_ref[pl.ds(2 * pair, 32, stride=4), :] = image
+        rows_ref[pl.ds(2 * pair + 1, 32, stride=4), :] = pltpu.roll(image, 64, 1)
+    out_ref[...] = rows_ref[...].T[:STRIP]
+    for pair in range(2):
+        half_copy(pair).wait_send()
+        for d in (1, 3, 2):
+            part_copy(pair, d).wait_send()
 
 
 def body(visibilities, weights, cell_index, kernel_index, layer_index, tile_counts, kernel_table, layer_depth):
-    rows = slot_rows(visibilities[0], weights[0], cell_index[0], kernel_index[0], layer_index[0], tile_counts[0])
-    buf = lax.all_to_all(jnp.broadcast_to(rows[None], (16, 8, SLOTS)), "bl", 0, 0, tiled=True)
     fh, fl = dft_tables()
-    vmem = pl.BlockSpec(memory_space=pltpu.VMEM)
-    packed, squares = pl.pallas_call(
-        compute_kernel,
-        out_shape=(jax.ShapeDtypeStruct((2, 256, 128), F32), jax.ShapeDtypeStruct((8, SLOTS), F32)),
-        in_specs=[vmem, vmem, pl.BlockSpec(memory_space=pltpu.SMEM), vmem, vmem],
-        out_specs=(vmem, vmem),
+    far = pl.BlockSpec(memory_space=pl.ANY)
+    wide = SLOTS * max(GROUPS)
+    vmem, smem, dma = pltpu.VMEM, pltpu.SMEM, pltpu.SemaphoreType.DMA
+    return pl.pallas_call(
+        kernel,
+        out_shape=jax.ShapeDtypeStruct((STRIP, 128), F32),
+        in_specs=[far] * 10,
+        out_specs=pl.BlockSpec(memory_space=pltpu.VMEM),
         scratch_shapes=[
-            pltpu.VMEM((400, 256), BF16),
-            pltpu.VMEM((GRID, SLOTS), BF16),
-            pltpu.VMEM((GRID, SLOTS), BF16),
-            pltpu.VMEM((GRID, 256), F32),
-            pltpu.VMEM((4, 256, 128), F32),
-            pltpu.VMEM((4, 256, 128), F32),
+            smem((1, 2), I32),
+            smem((2,), F32),
+            vmem((1, 2, 2, 128), F32),
+            vmem((1, 2, 128), F32),
+            vmem((1, 2, 128), I32),
+            vmem((1, 2, 128), I32),
+            vmem((1, 2, 128), I32),
+            vmem((SUPPORT, OVERSAMPLE), F32),
+            vmem((4, 512, 256), BF16),
+            vmem((4, 512, 256), BF16),
+            vmem((16, 8, SLOTS), F32),
+            vmem((400, 256), BF16),
+            *([vmem((256, wide), BF16)] * 2 + [vmem((GRID, wide), BF16)] * 2) * 2,
+            vmem((GRID, 256), F32),
+            vmem((4, 256, 128), F32),
+            vmem((4, 256, 128), F32),
+            vmem((2, 4, 40, 128), F32),
+            vmem((2, 4, 32, 128), F32),
+            vmem((4, 40, 128), F32),
+            vmem((4, 32, 128), F32),
+            vmem((4, 40, 128), F32),
+            vmem((4, 32, 128), F32),
+            vmem((4, 40, 128), F32),
+            vmem((4, 32, 128), F32),
+            vmem((128, 128), F32),
+            dma((10,)),
+            dma((16,)),
+            dma((16,)),
+            dma((2,)),
+            dma((2,)),
+            dma((2, 4)),
+            dma((2, 4)),
         ],
-    )(buf, kernel_table, layer_depth, jnp.asarray(fh), jnp.asarray(fl))
-    total = jnp.sum(squares[0])
-    blocks = packed.reshape(2, 8, 32, 128).transpose(1, 0, 2, 3).reshape(8, 64, 128)
-    blocks = jnp.concatenate([blocks, jnp.full((8, 8, 128), total)], axis=1)
-    got = lax.all_to_all(blocks, "wa", 0, 0, tiled=True).sum(axis=0)
-    image = got[:64].reshape(2, 32, 2, 64).transpose(1, 0, 2, 3).reshape(128, 64)
-    return image / jnp.sqrt(got[64, 0])
+        compiler_params=pltpu.CompilerParams(
+            collective_id=0, has_side_effects=True, vmem_limit_bytes=VMEM_MIB * 1024 * 1024
+        ),
+    )(
+        tile_counts, layer_depth, visibilities, weights, cell_index, kernel_index, layer_index, kernel_table.T,
+        jnp.asarray(fh), jnp.asarray(fl),
+    ).T
 
 
 def solution(mesh):

time: 60 us -> 29.6 us (0.49)
  blocking collectives: 14.3 us -> 0 us
  Pallas kernels: 20.2 us -> 28 us
  starting transfers between devices: 7.7 us -> 0 us
  waiting for transfers between devices: 6.18 us -> 0 us
  local copies, waits for them, and re-layouts: 6.98 us -> 1.38 us
  other arithmetic: 3.38 us -> 0 us
  between operations: 0.8 us -> 0.01 us
    all_to_all x1 -> x0, blocking collectives: 14.3 us -> none  [body(): got = lax.all_to_all(blocks, 'wa', 0, 0, tiled=True).sum(axis=0)]
    pallas_call x1, Pallas kernels: 20.2 us -> 28 us  [body(): pl.pallas_call(kernel, out_shape=jax.ShapeDtypeStruct((STRIP, 128), F32),...]
    all_to_all x1 -> x0, starting transfers between devices: 7.7 us -> none  [body(): lax.all_to_all(jnp.broadcast_to(rows[None], (16, 8, SLOTS)), 'bl', 0, 0,...]
    all_to_all x1 -> x0, waiting for transfers between devices: 6.18 us -> none  [body(): lax.all_to_all(jnp.broadcast_to(rows[None], (16, 8, SLOTS)), 'bl', 0, 0,...]
    reduce_sum x2 -> x0, other arithmetic: 1.32 us -> none  [the longest x1 1.3 us: body(): total = jnp.sum(squares[0])]
    unnamed x15 -> x1, local copies, waits for them, and re-layouts: 2.68 us -> 1.38 us
    mul x2 -> x0, other arithmetic: 1.28 us -> none  [the longest x1 1.27 us: slot_rows(): vis[t, 1:2] * used]
    slice x2 -> x0, local copies, waits for them, and re-layouts: 1.15 us -> none  [the longest x1 0.63 us: slot_rows(): used = jnp.where(lane < counts[t], weights[t:t + 1], 0.0)]
  transfers between devices with their start and end apart: 1 -> 0, of which waited for: 1 -> 0; matrix products, arithmetic and copies ran while one was open for 1% -> 0% of each run, Pallas kernels for 0% -> 0%
where the time goes in v2:
time: 29.6 us; the launch traced here: 29.4 us
  Pallas kernels  28 us (95%)
  local copies, waits for them, and re-layouts  1.38 us (5%)
    pallas_call x1, Pallas kernels, body(): pl.pallas_call(kernel, out_shape=jax.ShapeDtypeStruct((STRIP, 128), F32),...  28 us
    unnamed x1, local copies, waits for them, and re-layouts  1.38 us

profile of v2, /device:TPU:1, one launch (start us, length us, event | category | flops | bytes accessed | tf_op | source)
XLA Modules:
  0.0 29.4 jit_solution(1462657459670757448)
XLA Ops:
  0.0 28.0 %shard_map.100 = f32[64,128]{1,0:T(8,128)} custom-call(s32[1,2]{1,0:T(1,128)} %counts_hbm.1, f32[2]{0:T(128)} %depth_hbm.1, f32[1,2,2,128]{3,2,1,0:T(2,128)} %vis_hbm.1, f32[1,2,128]{2,1,0:T(2,128)} %weights_hbm.1, s32[1,2,128]{2,1,0:T(2,128)} %cell_hbm.1, s32[1,2,128]{2,1,0:T(2,128)} %kern_hbm.1, s32[1,2,128]{2,1,0:T(2,128)} %layer_hbm.1, f32[8,16]{1,0:T(8,128)} %bitcast.3, ...), custom_call_target="tpu_custom_call" | custom-call | tf_op jit(solution)/shard_map/pallas_call | solution.py:393
  28.0 1.4 %copy.12 = f32[128,64]{0,1:T(8,128)} copy(f32[128,64]{0,1:T(8,128)} %bitcast.2) | data formatting | bytes 65536

commit v3 on v2

--- a/solution.py
+++ b/solution.py
@@ -14,10 +14,11 @@
 STRIP = 64
 SLOTS = 256
 FIELD = 0.6
+LAG = 4
 MIX = 0
-GROUPS = (1,2,3,3,3,3)
+GROUPS = (1,1,2,3,4,4)
 MROWS = 256
-VMEM_MIB = 60
+VMEM_MIB = 40
 NT = (((1,), (1,)), ((), ()))
 NN = (((1,), (0,)), ((), ()))
 TN = (((0,), (0,)), ((), ()))
@@ -166,9 +167,10 @@
     hot = jnp.concatenate(
         [hot1, hot1, hot0, hot0, hotv, hotv, hotu, jnp.zeros((80, SLOTS), BF16)], axis=0
     )
-    found = dot(tables_ref[...], hot)
-    ar, ai, br, bi, kr, ki = (found[64 * i : 64 * i + 64] for i in range(6))
-    ku_high, ku_low = found[384:392], found[392:400]
+    found, rest = dot(tables_ref[0:192], hot), dot(tables_ref[192:400], hot)
+    ar, ai, br = (found[64 * i : 64 * i + 64] for i in range(3))
+    bi, kr, ki = (rest[64 * i : 64 * i + 64] for i in range(3))
+    ku_high, ku_low = rest[192:200], rest[200:208]
     vr, vi = wr * kr - wi * ki, wr * ki + wi * kr
     cr, ci = ar * br - ai * bi, ar * bi + ai * br
     pr, pi = vr * cr - vi * ci, vr * ci + vi * cr
@@ -219,23 +221,27 @@
     acc_ref[rows] = added if first else acc_ref[rows] + added
 
 
-def transform(acc_ref, fh_ref, fl_ref, cos_ref, sin_ref, store):
+def turned_rows(acc_ref):
     g = [acc_ref[256 * i : 256 * i + 256] for i in range(4)]
     s02, d02, s13, d13 = g[0] + g[2], g[0] - g[2], g[1] + g[3], g[1] - g[3]
     turned = jnp.concatenate([-d13[:, 128:], d13[:, :128]], axis=1)
-    mixed = [s02 + s13, d02 + turned, s02 - s13, d02 - turned]
-    lane = iota((256, 128), 1)
-    for pair in range(2):
-        sums = []
-        for xi in (2 * pair, 2 * pair + 1):
-            high, low = split(mixed[xi])
-            fh, fl = fh_ref[xi], fl_ref[xi]
-            p = dot(fh, high) + dot(fh, low) + dot(fl, high)
-            re = p[:256, :128] - p[256:, 128:]
-            im = p[256:, :128] + p[:256, 128:]
-            scr = re * cos_ref[xi] - im * sin_ref[xi]
-            sums.append(scr + pltpu.roll(scr, 64, 1))
-        store(pair, jnp.where(lane < 64, sums[0], sums[1]))
+    return [s02 + s13, d02 + turned, s02 - s13, d02 - turned]
+
+
+def row_products(xi, mixed, fh_ref, fl_ref):
+    high, low = split(mixed[xi])
+    out = []
+    for rows in (slice(0, 256), slice(256, 512)):
+        fh, fl = fh_ref[xi, rows], fl_ref[xi, rows]
+        out.append(dot(fh, high) + dot(fh, low) + dot(fl, high))
+    return out
+
+
+def screened_rows(xi, p, cos_ref, sin_ref):
+    re = p[0][:, :128] - p[1][:, 128:]
+    im = p[1][:, :128] + p[0][:, 128:]
+    scr = re * cos_ref[xi] - im * sin_ref[xi]
+    return scr + pltpu.roll(scr, 64, 1)
 
 
 def mesh_offsets():
@@ -261,7 +267,7 @@
     out_ref,
     counts_ref, depth_ref, vis_ref, weights_ref, cell_ref, kern_ref, layer_ref, table_ref, fh_ref, fl_ref,
     buf, tables_ref, vh0, vl0, high0, low0, vh1, vl1, high1, low1, acc_ref, cos_ref, sin_ref,
-    send0, send1, half0, half1, red0, red1, got0, got1, rows_ref,
+    send_ref, half_ref, red_ref, got_ref, sq_ref, sq_half, sq_red, sq_got, rows_ref,
     load_sem, slot_send, slot_recv, half_send, half_recv, part_send, part_recv,
 ):
     bl, wa = lax.axis_index("bl"), lax.axis_index("wa")
@@ -294,10 +300,6 @@
         )
         for k in range(1, 16)
     ]
-    pl.semaphore_wait(barrier, 19)
-    for copy in copies[::-1]:
-        copy.start()
-
     first_y = bl * STRIP
     loads[7].wait()
     tables_ref[...] = make_tables(first_y, table_ref[...])
@@ -307,6 +309,9 @@
     fill_operands(0, own, tables_ref, *operands[0])
     for m in range(0, GRID, MROWS):
         add_rows(m, 1, True, acc_ref, *operands[0])
+    pl.semaphore_wait(barrier, 19)
+    for copy in copies[::-1]:
+        copy.start()
     loads[6].wait()
     make_screen(first_y, (depth_ref[0], depth_ref[1]), cos_ref, sin_ref)
     k, ready = 1, 0
@@ -326,63 +331,78 @@
         k, ready = k + count, count
     for m in range(0, GRID, MROWS):
         add_rows(m, ready, False, acc_ref, *operands[len(GROUPS) % 2])
-    squares = squares[:, :128] + squares[:, 128:]
-    for copy in copies:
-        copy.wait_send()
-    for load in loads[8:]:
-        load.wait()
-
-    sends, halves, reds, gots = (send0, send1), (half0, half1), (red0, red1), (got0, got1)
-
-    def half_copy(pair):
+    def half_copy(n):
         return pltpu.make_async_remote_copy(
-            src_ref=sends[pair].at[1 - core],
-            dst_ref=halves[pair],
-            send_sem=half_send.at[pair],
-            recv_sem=half_recv.at[pair],
+            src_ref=send_ref.at[n, 1 - core] if n < 4 else sq_ref,
+            dst_ref=half_ref.at[n] if n < 4 else sq_half,
+            send_sem=half_send.at[n],
+            recv_sem=half_recv.at[n],
             device_id=sibling,
             device_id_type=MESH,
         )
 
-    def part_copy(pair, d):
+    def part_copy(n, d):
         return pltpu.make_async_remote_copy(
-            src_ref=reds[pair].at[(z + d) % 4],
-            dst_ref=gots[pair].at[d],
-            send_sem=part_send.at[pair, d],
-            recv_sem=part_recv.at[pair, d],
+            src_ref=red_ref.at[n, (z + d) % 4] if n < 4 else sq_red,
+            dst_ref=got_ref.at[n, d] if n < 4 else sq_got.at[d],
+            send_sem=part_send.at[n, d],
+            recv_sem=part_recv.at[n, d],
             device_id=z_peer[d],
             device_id_type=MESH,
         )
 
-    def store(pair, value):
+    def pass_on(n):
+        half_copy(n).wait_recv()
+        if n < 4:
+            red_ref[n] = send_ref[n, core] + half_ref[n]
+        else:
+            sq_red[...] = sq_ref[...] + sq_half[...]
+        for d in (2, 1, 3):
+            part_copy(n, d).start()
+
+    sq_ref[...] = jnp.broadcast_to(squares[:, :128] + squares[:, 128:], (8, 128))
+    for load in loads[8:]:
+        load.wait()
+    half_copy(4).start()
+    left = iota((16, 128), 1) < STRIP
+    mixed = turned_rows(acc_ref)
+    coming = row_products(0, mixed, fh_ref, fl_ref)
+    for xi in range(4):
+        now = coming
+        if xi < 3:
+            coming = row_products(xi + 1, mixed, fh_ref, fl_ref)
+        value = screened_rows(xi, now, cos_ref, sin_ref)
         for w in range(8):
-            sends[pair][w % 2, w // 2, 0:32] = value[32 * w : 32 * w + 32]
-        if pair == 0:
-            send0[:, :, 32:40] = jnp.broadcast_to(squares[None, None], (2, 4, 8, 128))
-        half_copy(pair).start()
-
-    transform(acc_ref, fh_ref, fl_ref, cos_ref, sin_ref, store)
-    for pair in range(2):
-        half_copy(pair).wait_recv()
-        reds[pair][...] = sends[pair][core] + halves[pair][...]
-        for d in (2, 1, 3):
-            part_copy(pair, d).start()
-    norm = None
-    for pair in range(2):
-        total = reds[pair][z]
+            x = 32 * w
+            send_ref[xi, w % 2, w // 2] = jnp.where(left, value[x : x + 16], value[x + 16 : x + 32])
+        half_copy(xi).start()
+        if xi == 1:
+            pass_on(4)
+        if xi >= LAG:
+            pass_on(xi - LAG)
+    for xi in range(4 - LAG, 4):
+        pass_on(xi)
+
+    total = sq_red[...]
+    for d in (1, 3, 2):
+        part_copy(4, d).wait_recv()
+        total = total + sq_got[d]
+    norm = lax.rsqrt(jnp.sum(total[0:1], axis=1, keepdims=True))
+    for xi in range(4):
+        total = red_ref[xi, z]
         for d in (1, 3, 2):
-            part_copy(pair, d).wait_recv()
-            total = total + gots[pair][d]
-        if pair == 0:
-            norm = lax.rsqrt(jnp.sum(total[32:33], axis=1, keepdims=True))
-        image = total[0:32] * norm
-        rows_ref[pl.ds(2 * pair, 32, stride=4), :] = image
-        rows_ref[pl.ds(2 * pair + 1, 32, stride=4), :] = pltpu.roll(image, 64, 1)
+            part_copy(xi, d).wait_recv()
+            total = total + got_ref[xi, d]
+        image = total * norm
+        rows_ref[pl.ds(xi, 16, stride=4), :] = image
+        rows_ref[pl.ds(64 + xi, 16, stride=4), :] = pltpu.roll(image, 64, 1)
     out_ref[...] = rows_ref[...].T[:STRIP]
-    for pair in range(2):
-        half_copy(pair).wait_send()
+    for copy in copies:
+        copy.wait_send()
+    for n in range(5):
+        half_copy(n).wait_send()
         for d in (1, 3, 2):
-            part_copy(pair, d).wait_send()
+            part_copy(n, d).wait_send()
 
 
 def body(visibilities, weights, cell_index, kernel_index, layer_index, tile_counts, kernel_table, layer_depth):
@@ -412,29 +432,34 @@
             vmem((GRID, 256), F32),
             vmem((4, 256, 128), F32),
             vmem((4, 256, 128), F32),
-            vmem((2, 4, 40, 128), F32),
-            vmem((2, 4, 32, 128), F32),
-            vmem((4, 40, 128), F32),
-            vmem((4, 32, 128), F32),
-            vmem((4, 40, 128), F32),
-            vmem((4, 32, 128), F32),
-            vmem((4, 40, 128), F32),
-            vmem((4, 32, 128), F32),
+            vmem((4, 2, 4, 16, 128), F32),
+            vmem((4, 4, 16, 128), F32),
+            vmem((4, 4, 16, 128), F32),
+            vmem((4, 4, 16, 128), F32),
+            vmem((8, 128), F32),
+            vmem((8, 128), F32),
+            vmem((8, 128), F32),
+            vmem((4, 8, 128), F32),
             vmem((128, 128), F32),
             dma((10,)),
             dma((16,)),
             dma((16,)),
-            dma((2,)),
-            dma((2,)),
-            dma((2, 4)),
-            dma((2, 4)),
+            dma((5,)),
+            dma((5,)),
+            dma((5, 4)),
+            dma((5, 4)),
         ],
         compiler_params=pltpu.CompilerParams(
             collective_id=0, has_side_effects=True, vmem_limit_bytes=VMEM_MIB * 1024 * 1024
         ),
     )(
-        tile_counts, layer_depth, visibilities, weights, cell_index, kernel_index, layer_index, kernel_table.T,
-        jnp.asarray(fh), jnp.asarray(fl),
+        *(
+            pltpu.with_memory_space_constraint(value, pltpu.HBM)
+            for value in (
+                tile_counts, layer_depth, visibilities, weights, cell_index, kernel_index, layer_index,
+                kernel_table.T, jnp.asarray(fh), jnp.asarray(fl),
+            )
+        )
     ).T
 
 

time: 29.6 us -> 27.5 us (0.929)
  Pallas kernels: 28 us -> 26.8 us
  local copies, waits for them, and re-layouts: 1.38 us -> 0.62 us
    pallas_call x1, Pallas kernels: 28 us -> 26.8 us  [body(): pl.pallas_call(kernel, out_shape=jax.ShapeDtypeStruct((STRIP, 128), F32),...]
    unnamed x1, local copies, waits for them, and re-layouts: 1.38 us -> 0.62 us
where the time goes in v3:
time: 27.5 us; the launch traced here: 27.4 us
  Pallas kernels  26.8 us (97%)
  local copies, waits for them, and re-layouts  0.62 us (2%)
    pallas_call x1, Pallas kernels, body(): pl.pallas_call(kernel, out_shape=jax.ShapeDtypeStruct((STRIP, 128), F32),...  26.8 us
    unnamed x1, local copies, waits for them, and re-layouts  0.62 us

profile of v3, /device:TPU:1, one launch (start us, length us, event | category | flops | bytes accessed | tf_op | source)
XLA Modules:
  0.0 27.4 jit_solution(646660554718706570)
XLA Ops:
  0.0 26.8 %shard_map.100 = f32[64,128]{1,0:T(8,128)S(1)} custom-call(s32[1,2]{1,0:T(1,128)} %counts_hbm.1, f32[2]{0:T(128)} %depth_hbm.1, f32[1,2,2,128]{3,2,1,0:T(2,128)} %vis_hbm.1, f32[1,2,128]{2,1,0:T(2,128)} %weights_hbm.1, s32[1,2,128]{2,1,0:T(2,128)} %cell_hbm.1, s32[1,2,128]{2,1,0:T(2,128)} %kern_hbm.1, s32[1,2,128]{2,1,0:T(2,128)} %layer_hbm.1, ...), custom_call_target="tpu_custom_call" | custom-call | tf_op jit(solution)/shard_map/pallas_call | solution.py:413
  26.8 0.6 %copy.12 = f32[128,64]{0,1:T(8,128)} copy(f32[128,64]{0,1:T(8,128)S(1)} %bitcast.2) | data formatting | bytes 65536

commit v4 on v3

--- a/solution.py
+++ b/solution.py
@@ -16,7 +16,7 @@
 FIELD = 0.6
 LAG = 4
 MIX = 0
-GROUPS = (1,1,2,3,4,4)
+GROUPS = (3,3,4,5)
 MROWS = 256
 VMEM_MIB = 40
 NT = (((1,), (1,)), ((), ()))
@@ -98,8 +98,8 @@
 
 
 def make_tables(first_y, table):
-    lane = iota((STRIP, 256), 1)
-    y = first_y + iota((STRIP, 256), 0)
+    lane, line = iota((16, 256), 1), iota((16, 256), 0)
+    y = jnp.where(line < 8, first_y + 8 * line, line - 8)
     low5 = lane & 31
     step = jnp.where(lane < 64, 32 * low5, low5)
     turns = ((y * step) & (GRID - 1)).astype(F32) * (1.0 / GRID)
@@ -112,6 +112,7 @@
             in_high = (lane >= first) & (lane < first + 32)
             in_low = (lane >= first + 32) & (lane < first + 64)
             pieces.append(jnp.where(in_high, high, jnp.where(in_low, low, 0.0)))
+    lane = iota((STRIP, 256), 1)
     wide = iota((OVERSAMPLE, 256), 1)
     pick = ((wide & 15) == iota((OVERSAMPLE, 256), 0)).astype(F32)
     spread = dot(table, pick, NN, lax.Precision.HIGHEST)
@@ -167,13 +168,16 @@
     hot = jnp.concatenate(
         [hot1, hot1, hot0, hot0, hotv, hotv, hotu, jnp.zeros((80, SLOTS), BF16)], axis=0
     )
-    found, rest = dot(tables_ref[0:192], hot), dot(tables_ref[192:400], hot)
-    ar, ai, br = (found[64 * i : 64 * i + 64] for i in range(3))
-    bi, kr, ki = (rest[64 * i : 64 * i + 64] for i in range(3))
-    ku_high, ku_low = rest[192:200], rest[200:208]
-    vr, vi = wr * kr - wi * ki, wr * ki + wi * kr
-    cr, ci = ar * br - ai * bi, ar * bi + ai * br
-    pr, pi = vr * cr - vi * ci, vr * ci + vi * cr
+    found, rest = dot(tables_ref[0:128], hot), dot(tables_ref[128:208], hot)
+    ar, ai, br, bi = (found[16 * i : 16 * i + 16] for i in range(4))
+    kr, ki = found[64:128], rest[0:64]
+    ku_high, ku_low = rest[64:72], rest[72:80]
+    tr, ti = ar * br - ai * bi, ar * bi + ai * br
+    er, ei = wr * tr[:8] - wi * ti[:8], wr * ti[:8] + wi * tr[:8]
+    fr, fi = tr[8:], ti[8:]
+    cr = jnp.concatenate([er[i : i + 1] * fr - ei[i : i + 1] * fi for i in range(8)], axis=0)
+    ci = jnp.concatenate([er[i : i + 1] * fi + ei[i : i + 1] * fr for i in range(8)], axis=0)
+    pr, pi = kr * cr - ki * ci, kr * ci + ki * cr
     second = lay.astype(BF16)
     first = (1.0 - lay).astype(BF16)
     rh, rl = split(pr)
@@ -181,33 +185,32 @@
     v_high = jnp.concatenate([rh * first, rh * second, ih * first, ih * second], axis=0)
     v_low = jnp.concatenate([rl * first, rl * second, il * first, il * second], axis=0)
 
-    d = iota((16, SLOTS), 0) - inner
-    zero = jnp.zeros((16, SLOTS), F32)
+    d = (iota((16, SLOTS), 0) - inner).astype(F32).astype(BF16)
+    zero = jnp.zeros((16, SLOTS), BF16)
     lows, highs = [zero, zero], [zero, zero]
     for a in range(SUPPORT):
-        here, past = d == a, d == a - 16
+        here, past = d == jnp.asarray(a, BF16), d == jnp.asarray(a - 16, BF16)
         for i, ku in enumerate((ku_high, ku_low)):
-            lows[i] = jnp.where(here, ku[a : a + 1], lows[i])
-            highs[i] = jnp.where(past, ku[a : a + 1], highs[i])
-    lows = [v.astype(BF16) for v in lows]
-    highs = [v.astype(BF16) for v in highs]
+            tap = jnp.broadcast_to(ku[a : a + 1], (16, SLOTS)).astype(BF16)
+            lows[i] = jnp.where(here, tap, lows[i])
+            highs[i] = jnp.where(past, tap, highs[i])
     blk = jnp.broadcast_to(block.astype(F32), (16, SLOTS)).astype(BF16)
-    nxt = jnp.broadcast_to(((block + 1) & 63).astype(F32), (16, SLOTS)).astype(BF16)
-    return v_high, v_low, lows, highs, blk, nxt
+    return v_high, v_low, lows, highs, blk
 
 
 def fill_operands(n, data, tables_ref, vh_ref, vl_ref, high_ref, low_ref):
     none = jnp.zeros((16, SLOTS), BF16)
     lanes = slice(SLOTS * n, SLOTS * n + SLOTS)
-    v_high, v_low, lows, highs, blk, nxt = slot_factors(data, tables_ref)
+    v_high, v_low, lows, highs, blk = slot_factors(data, tables_ref)
     vh_ref[:, lanes] = v_high
     vl_ref[:, lanes] = v_low
+    before = blk == jnp.asarray(63, BF16)
     for q in range(64):
         at = blk == jnp.asarray(q, BF16)
-        after = nxt == jnp.asarray(q, BF16)
         rows = slice(16 * q, 16 * q + 16)
-        high_ref[rows, lanes] = jnp.where(at, lows[0], jnp.where(after, highs[0], none))
-        low_ref[rows, lanes] = jnp.where(at, lows[1], jnp.where(after, highs[1], none))
+        high_ref[rows, lanes] = jnp.where(at, lows[0], jnp.where(before, highs[0], none))
+        low_ref[rows, lanes] = jnp.where(at, lows[1], jnp.where(before, highs[1], none))
+        before = at
 
 
 def add_rows(m, count, first, acc_ref, vh_ref, vl_ref, high_ref, low_ref):
@@ -246,7 +249,7 @@
 
 def mesh_offsets():
     near = lambda d: min(d, 4 - d)
-    return sorted(((dx, dy) for dx in range(4) for dy in range(4)), key=lambda o: near(o[0]) + near(o[1]))
+    return sorted(((dx, dy) for dx in range(4) for dy in range(4)), key=lambda o: (0 not in o, near(o[0]) + near(o[1])))
 
 
 OFFSETS = mesh_offsets()
@@ -268,7 +271,7 @@
     counts_ref, depth_ref, vis_ref, weights_ref, cell_ref, kern_ref, layer_ref, table_ref, fh_ref, fl_ref,
     buf, tables_ref, vh0, vl0, high0, low0, vh1, vl1, high1, low1, acc_ref, cos_ref, sin_ref,
     send_ref, half_ref, red_ref, got_ref, sq_ref, sq_half, sq_red, sq_got, rows_ref,
-    load_sem, slot_send, slot_recv, half_send, half_recv, part_send, part_recv,
+    load_sem, slot_send, slot_recv, half_send, half_recv, part_send, part_recv, line_sem,
 ):
     bl, wa = lax.axis_index("bl"), lax.axis_index("wa")
     bx, by, z, core = bl // 4, bl % 4, wa // 2, wa % 2
@@ -277,7 +280,8 @@
     sibling = {"wa": z * 2 + (1 - core)}
 
     barrier = pltpu.get_barrier_semaphore()
-    for peer in strips[:0:-1] + z_peer[1:] + [sibling]:
+    line = [k for k in range(1, 16) if 0 in OFFSETS[k]]
+    for peer in [strips[k] for k in line] + z_peer[1:] + [sibling]:
         pl.semaphore_signal(barrier, inc=1, device_id=peer, device_id_type=MESH)
     sources = (vis_hbm, weights_hbm, cell_hbm, kern_hbm, layer_hbm, counts_hbm, depth_hbm, table_hbm, fh_hbm, fl_hbm)
     targets = (vis_ref, weights_ref, cell_ref, kern_ref, layer_ref, counts_ref, depth_ref, table_ref, fh_ref, fl_ref)
@@ -300,6 +304,12 @@
         )
         for k in range(1, 16)
     ]
+    pl.semaphore_wait(barrier, 10)
+    for k in line:
+        if OFFSETS[k][1] == 0:
+            pl.semaphore_signal(line_sem, inc=1, device_id=strips[k], device_id_type=MESH)
+    for k in line:
+        copies[k - 1].start()
     first_y = bl * STRIP
     loads[7].wait()
     tables_ref[...] = make_tables(first_y, table_ref[...])
@@ -309,9 +319,10 @@
     fill_operands(0, own, tables_ref, *operands[0])
     for m in range(0, GRID, MROWS):
         add_rows(m, 1, True, acc_ref, *operands[0])
-    pl.semaphore_wait(barrier, 19)
-    for copy in copies[::-1]:
-        copy.start()
+    pl.semaphore_wait(line_sem, 3)
+    for k in range(15, 0, -1):
+        if k not in line:
+            copies[k - 1].start()
     loads[6].wait()
     make_screen(first_y, (depth_ref[0], depth_ref[1]), cos_ref, sin_ref)
     k, ready = 1, 0
@@ -427,7 +438,7 @@
             vmem((4, 512, 256), BF16),
             vmem((4, 512, 256), BF16),
             vmem((16, 8, SLOTS), F32),
-            vmem((400, 256), BF16),
+            vmem((208, 256), BF16),
             *([vmem((256, wide), BF16)] * 2 + [vmem((GRID, wide), BF16)] * 2) * 2,
             vmem((GRID, 256), F32),
             vmem((4, 256, 128), F32),
@@ -448,6 +459,7 @@
             dma((5,)),
             dma((5, 4)),
             dma((5, 4)),
+            pltpu.SemaphoreType.REGULAR,
         ],
         compiler_params=pltpu.CompilerParams(
             collective_id=0, has_side_effects=True, vmem_limit_bytes=VMEM_MIB * 1024 * 1024

time: 27.5 us -> 26.8 us (0.975)
  Pallas kernels: 26.8 us -> 26 us
    pallas_call x1, Pallas kernels: 26.8 us -> 26 us  [body(): pl.pallas_call(kernel, out_shape=jax.ShapeDtypeStruct((STRIP, 128), F32),...]
where the time goes in v4:
time: 26.8 us; the launch traced here: 26.6 us
  Pallas kernels  26 us (97%)
  local copies, waits for them, and re-layouts  0.62 us (2%)
    pallas_call x1, Pallas kernels, body(): pl.pallas_call(kernel, out_shape=jax.ShapeDtypeStruct((STRIP, 128), F32),...  26 us
    unnamed x1, local copies, waits for them, and re-layouts  0.62 us

profile of v4, /device:TPU:1, one launch (start us, length us, event | category | flops | bytes accessed | tf_op | source)
XLA Modules:
  0.0 26.6 jit_solution(1679110257363276766)
XLA Ops:
  0.0 26.0 %shard_map.100 = f32[64,128]{1,0:T(8,128)S(1)} custom-call(s32[1,2]{1,0:T(1,128)} %counts_hbm.1, f32[2]{0:T(128)} %depth_hbm.1, f32[1,2,2,128]{3,2,1,0:T(2,128)} %vis_hbm.1, f32[1,2,128]{2,1,0:T(2,128)} %weights_hbm.1, s32[1,2,128]{2,1,0:T(2,128)} %cell_hbm.1, s32[1,2,128]{2,1,0:T(2,128)} %kern_hbm.1, s32[1,2,128]{2,1,0:T(2,128)} %layer_hbm.1, ...), custom_call_target="tpu_custom_call" | custom-call | tf_op jit(solution)/shard_map/pallas_call | solution.py:424
  26.0 0.6 %copy.12 = f32[128,64]{0,1:T(8,128)} copy(f32[128,64]{0,1:T(8,128)S(1)} %bitcast.2) | data formatting | bytes 65536

commit v5 on v4

--- a/solution.py
+++ b/solution.py
@@ -394,17 +394,13 @@
     for xi in range(4 - LAG, 4):
         pass_on(xi)
 
-    total = sq_red[...]
-    for d in (1, 3, 2):
-        part_copy(4, d).wait_recv()
-        total = total + sq_got[d]
+    for n in (4, 0, 1, 2, 3):
+        for d in (1, 3, 2):
+            part_copy(n, d).wait_recv()
+    total = sq_red[...] + sq_got[1] + sq_got[3] + sq_got[2]
     norm = lax.rsqrt(jnp.sum(total[0:1], axis=1, keepdims=True))
     for xi in range(4):
-        total = red_ref[xi, z]
-        for d in (1, 3, 2):
-            part_copy(xi, d).wait_recv()
-            total = total + got_ref[xi, d]
-        image = total * norm
+        image = (red_ref[xi, z] + got_ref[xi, 1] + got_ref[xi, 3] + got_ref[xi, 2]) * norm
         rows_ref[pl.ds(xi, 16, stride=4), :] = image
         rows_ref[pl.ds(64 + xi, 16, stride=4), :] = pltpu.roll(image, 64, 1)
     out_ref[...] = rows_ref[...].T[:STRIP]

time: 26.8 us -> 26.8 us (level)
  no operation moved by 1% of the time
where the time goes in v5:
time: 26.8 us; the launch traced here: 26.7 us
  Pallas kernels  26.1 us (97%)
  local copies, waits for them, and re-layouts  0.62 us (2%)
    pallas_call x1, Pallas kernels, body(): pl.pallas_call(kernel, out_shape=jax.ShapeDtypeStruct((STRIP, 128), F32),...  26.1 us
    unnamed x1, local copies, waits for them, and re-layouts  0.62 us

profile of v5, /device:TPU:1, one launch (start us, length us, event | category | flops | bytes accessed | tf_op | source)
XLA Modules:
  0.0 26.7 jit_solution(5280491467471852935)
XLA Ops:
  0.0 26.1 %shard_map.100 = f32[64,128]{1,0:T(8,128)S(1)} custom-call(s32[1,2]{1,0:T(1,128)} %counts_hbm.1, f32[2]{0:T(128)} %depth_hbm.1, f32[1,2,2,128]{3,2,1,0:T(2,128)} %vis_hbm.1, f32[1,2,128]{2,1,0:T(2,128)} %weights_hbm.1, s32[1,2,128]{2,1,0:T(2,128)} %cell_hbm.1, s32[1,2,128]{2,1,0:T(2,128)} %kern_hbm.1, s32[1,2,128]{2,1,0:T(2,128)} %layer_hbm.1, ...), custom_call_target="tpu_custom_call" | custom-call | tf_op jit(solution)/shard_map/pallas_call | solution.py:420
  26.1 0.6 %copy.12 = f32[128,64]{0,1:T(8,128)} copy(f32[128,64]{0,1:T(8,128)S(1)} %bitcast.2) | data formatting | bytes 65536
